TPU v7x, 32 devices: a whole 2x2x4 slice. The times are simulated.
32 devices in a mesh: section: 8 (over y, x, core), expert: 4 (over z).
Axes of the slice: x: 2, y: 2, z: 4, core: 2. Of those that a mesh axis runs over, the one named last changes fastest.
Arguments:
- top_grad: bfloat16 [2, 64, 2048], P(None, 'expert'), may hold values from -6 to 6
- layer_input: bfloat16 [8, 2, 64, 2048], P('section', None, 'expert'), may hold values from -6 to 6
- expert_out: bfloat16 [8, 2, 64, 2, 2048], P('section', None, 'expert'), may hold values from -3 to 3
- router_w: float32 [8, 2048, 8], P('section'), may hold values from -0.375 to 0.375
- expert_ids: int32 [8, 2, 64, 2], P('section', None, 'expert'), may hold values from 0 to 7, as said below
- hidden: bfloat16 [8, 2, 32, 7168], P('section', None, None, 'expert'), may hold values from -0.59765625 to 0.59765625
- down_w: bfloat16 [8, 7168, 2048], P('section', 'expert'), may hold values from -0.0625 to 0.0625
Outputs:
- input_grad: bfloat16 [8, 2, 64, 2048], P('section', None, 'expert')
- router_grad: float32 [8, 2048, 8], P('section')
- hidden_grad: bfloat16 [8, 2, 32, 7168], P('section', None, None, 'expert')
- down_grad: bfloat16 [8, 7168, 2048], P('section', 'expert')
Inputs may be any that keep to these rules, and one draw needn't show every extreme that they name: `expert_ids`: the two experts of a token differ. In each micro-batch, the 16 tokens of one device choose expert 0 at most 8 times, and exactly 8 times in some blocks of every draw.
All inputs are finite; a program needn't handle non-finite values.
Results may differ from a plain program's by a relative error of at most 0.024.
Values may be sent and summed in bfloat16 or wider, within the bound.
A program may use at most 64 MiB of HBM per device.

v0:
```python
import jax
import jax.numpy as jnp
from jax import lax
from jax.sharding import PartitionSpec as P


def passed_along(value, axis, by):
    count = lax.axis_size(axis)
    pairs = [(i, i + by) for i in range(count) if 0 <= i + by < count]
    return lax.ppermute(value, axis, pairs)


def gate_pair(inputs, weights, chosen):
    logits = jnp.einsum(
        "mtd,de->mte", inputs.astype(jnp.float32), weights, precision=lax.Precision.HIGHEST
    )
    select = (chosen[..., None] == jnp.arange(weights.shape[1], dtype=jnp.int32)).astype(
        jnp.float32
    )
    picked = jnp.sum(select * logits[..., None, :], axis=-1)
    gate_first = jax.nn.sigmoid(picked[..., 0] - picked[..., 1])
    return (gate_first, select)


def backprop(cotangent, inputs, outputs, weights, select, gate_first):
    cot_float = cotangent.astype(jnp.float32)
    gate_dot = jnp.einsum("mtkd,mtd->mtk", outputs, cotangent, preferred_element_type=jnp.float32)
    logit_diff = gate_first * (1.0 - gate_first) * (gate_dot[..., 0] - gate_dot[..., 1])
    logit_grad = logit_diff[..., None] * (select[..., 0, :] - select[..., 1, :])
    passed = cot_float + jnp.einsum(
        "mte,de->mtd", logit_grad, weights, precision=lax.Precision.HIGHEST
    )
    router_part = jnp.einsum(
        "mtd,mte->de", inputs.astype(jnp.float32), logit_grad, precision=lax.Precision.HIGHEST
    )
    return (passed.astype(jnp.bfloat16), router_part)


def dispatch_rows(cotangent, gate_first, chosen, capacity):
    is_zero = (chosen == 0).astype(jnp.float32)
    zero_gate = gate_first * is_zero[..., 0] + (1.0 - gate_first) * is_zero[..., 1]
    routed = is_zero[..., 0] + is_zero[..., 1]
    slot_pos = (jnp.cumsum(routed, axis=-1) - routed).astype(jnp.int32)
    slot_ids = jnp.arange(capacity, dtype=jnp.int32)
    pick_table = (
        (slot_pos[..., None, :] == slot_ids[:, None]) & (routed[..., None, :] > 0.5)
    ).astype(jnp.float32)
    scaled = zero_gate[..., None] * cotangent.astype(jnp.float32)
    rows_out = jnp.einsum("mbcu,mbud->mbcd", pick_table, scaled, precision=lax.Precision.HIGHEST)
    return rows_out.astype(jnp.bfloat16)


def per_device(top_grad, layer_input, expert_out, router_w, expert_ids, hidden, down_w):
    section_count = lax.axis_size("section")
    section_index = lax.axis_index("section")
    micro_count = top_grad.shape[0]
    tok_rows = top_grad.shape[1]
    width = top_grad.shape[2]
    inputs = layer_input[0]
    saved_outs = expert_out[0]
    router = router_w[0]
    chosen = expert_ids[0]
    gate_first, select = gate_pair(inputs, router, chosen)
    is_last = section_index == section_count - 1
    empty_cot = jnp.zeros((micro_count, tok_rows, width), jnp.bfloat16)
    empty_router = jnp.zeros((width, router.shape[1]), jnp.float32)

    def advance_all(moment, totals):
        arrived, section_dy, section_dx, router_acc = totals
        active = moment == section_count - 1 - section_index
        cotangent = jnp.where(is_last, top_grad, arrived)
        passed, router_part = backprop(cotangent, inputs, saved_outs, router, select, gate_first)
        section_dy = jnp.where(active, cotangent, section_dy)
        section_dx = jnp.where(active, passed, section_dx)
        router_acc = router_acc + jnp.where(active, router_part, 0.0)
        arrived = passed_along(passed, "section", -1)
        return (arrived, section_dy, section_dx, router_acc)

    start_state = (empty_cot, empty_cot, empty_cot, empty_router)
    _, section_dy, section_dx, router_acc = lax.fori_loop(
        0, section_count, advance_all, start_state
    )
    total_tokens = micro_count * tok_rows * lax.axis_size("expert")
    router_grad = lax.psum(router_acc, "expert") / total_tokens
    capacity = tok_rows // 2
    rows_out = dispatch_rows(section_dy[:, None], gate_first[:, None], chosen[:, None], capacity)
    rows_out = rows_out.reshape(micro_count, capacity, width)
    saved_hidden = hidden[0]
    weight = down_w[0]
    ff_local = weight.shape[0]
    slot_total = saved_hidden.shape[1]
    gathered = lax.all_gather(rows_out, "expert", axis=1, tiled=True)
    flat_rows = gathered.reshape(-1, width)
    hidden_acc = lax.dot_general(
        flat_rows, weight, (((1,), (1,)), ((), ())), preferred_element_type=jnp.float32
    )
    hidden_acc = hidden_acc.astype(jnp.bfloat16).reshape(micro_count, slot_total, ff_local)
    weight_sum = lax.dot_general(
        saved_hidden.reshape(-1, ff_local),
        flat_rows,
        (((0,), (0,)), ((), ())),
        preferred_element_type=jnp.float32,
    )
    return (
        section_dx[None],
        router_grad[None],
        hidden_acc[None],
        weight_sum.astype(jnp.bfloat16)[None],
    )


def solution(mesh):
    placed = (
        P(None, "expert", None),
        P("section", None, "expert", None),
        P("section", None, "expert", None, None),
        P("section", None, None),
        P("section", None, "expert", None),
        P("section", None, None, "expert"),
        P("section", "expert", None),
    )
    return jax.shard_map(
        per_device,
        mesh=mesh,
        in_specs=placed,
        out_specs=(
            P("section", None, "expert", None),
            P("section", None, None),
            P("section", None, None, "expert"),
            P("section", "expert", None),
        ),
        check_vma=False,
    )
```

profile of v0, /device:TPU:0, one launch (start us, length us, event | category | flops | bytes accessed | tf_op | source)
XLA Modules:
  0.0 136.3 jit_solution(297032122991663004)
XLA Ops:
  8.0 1.5 %fusion.22 = f32[2,16,8]{1,2,0:T(8,128)S(1)} fusion(f32[1,2048,8]{1,2,0:T(8,128)} %param.12, bf16[1,2,16,2048]{3,2,1,0:T(8,128)(2,1)} %param.10), kind=kOutput, calls=%fused_computation.29 | convolution fusion | flops 6291456 | bytes 197632 | tf_op jit(solution)/shard_map/mtd,de->mte/dot_general | solution.py:14
  9.5 73.4 %while.22 = (s32[]{:T(128)}, bf16[2,16,2048]{2,1,0:T(8,128)(2,1)S(1)}, bf16[2,16,2048]{2,1,0:T(8,128)(2,1)S(1)}, bf16[2,16,2048]{2,1,0:T(8,128)(2,1)S(1)}, f32[2...) while((s32[]{:T(128)}, ...), condition=%wide.region_2.3_spmd.clone, body=%wide.region_1.2_spmd.clone.sunk | while | flops 13419140 | bytes 2428622 | solution.py:80
  9.7 1.6 %fusion.53 = f32[2,16,1,2]{3,2,1,0:T(1,128)S(1)} fusion(bf16[2,16,2,2048]{3,2,1,0:T(2,128)(2,1)} %get-tuple-element.510, bf16[2,16,2048,1]{2,1,0,3:T(8,128)(2,1)S(1)} %bitcast.83), kind=kOutput, calls=%fused_computation.6.clone.1 | convolution fusion | flops 262144 | bytes 393472 | tf_op jit(solution)/shard_map/while/body/eval_jaxpr/mtkd,mtd->mtk/dot_general | solution.py:27
  11.3 1.3 select_select_fusion.5
  12.6 1.3 collective-permute-start
  13.9 1.1 fusion.55
  15.1 0.8 collective-permute-done
  15.9 1.6 %fusion.53 = f32[2,16,1,2]{3,2,1,0:T(1,128)S(1)} fusion(bf16[2,16,2,2048]{3,2,1,0:T(2,128)(2,1)} %get-tuple-element.510, bf16[2,16,2048,1]{2,1,0,3:T(8,128)(2,1)S(1)} %bitcast.83), kind=kOutput, calls=%fused_computation.6.clone.1 | convolution fusion | flops 262144 | bytes 393472 | tf_op jit(solution)/shard_map/while/body/eval_jaxpr/mtkd,mtd->mtk/dot_general | solution.py:27
  17.6 1.3 select_select_fusion.5
  18.9 1.3 collective-permute-start
  20.2 1.1 fusion.55
  21.4 4.7 %collective-permute-done = bf16[2,16,2048]{2,1,0:T(8,128)(2,1)S(1)} collective-permute-done((bf16[2,16,2048]{2,1,0:T(8,128)(2,1)S(1)}, bf16[2,16,2048]{2,1,0:T(8,128)(2,1)S(1)}, u32[]{:S(2)}, u32[]{:S(2)}) %collective-permute-start) | collective-permute-done | bytes 131104 | tf_op jit(solution)/shard_map/while/body/eval_jaxpr/ppermute | solution.py:10
  26.1 1.6 %fusion.53 = f32[2,16,1,2]{3,2,1,0:T(1,128)S(1)} fusion(bf16[2,16,2,2048]{3,2,1,0:T(2,128)(2,1)} %get-tuple-element.510, bf16[2,16,2048,1]{2,1,0,3:T(8,128)(2,1)S(1)} %bitcast.83), kind=kOutput, calls=%fused_computation.6.clone.1 | convolution fusion | flops 262144 | bytes 393472 | tf_op jit(solution)/shard_map/while/body/eval_jaxpr/mtkd,mtd->mtk/dot_general | solution.py:27
  27.8 1.3 select_select_fusion.5
  29.1 1.3 collective-permute-start
  30.4 1.1 fusion.55
  31.6 3.8 %collective-permute-done = bf16[2,16,2048]{2,1,0:T(8,128)(2,1)S(1)} collective-permute-done((bf16[2,16,2048]{2,1,0:T(8,128)(2,1)S(1)}, bf16[2,16,2048]{2,1,0:T(8,128)(2,1)S(1)}, u32[]{:S(2)}, u32[]{:S(2)}) %collective-permute-start) | collective-permute-done | bytes 131104 | tf_op jit(solution)/shard_map/while/body/eval_jaxpr/ppermute | solution.py:10
  35.5 1.6 %fusion.53 = f32[2,16,1,2]{3,2,1,0:T(1,128)S(1)} fusion(bf16[2,16,2,2048]{3,2,1,0:T(2,128)(2,1)} %get-tuple-element.510, bf16[2,16,2048,1]{2,1,0,3:T(8,128)(2,1)S(1)} %bitcast.83), kind=kOutput, calls=%fused_computation.6.clone.1 | convolution fusion | flops 262144 | bytes 393472 | tf_op jit(solution)/shard_map/while/body/eval_jaxpr/mtkd,mtd->mtk/dot_general | solution.py:27
  37.2 1.3 select_select_fusion.5
  38.5 1.3 collective-permute-start
  39.8 1.1 fusion.55
  40.9 3.8 %collective-permute-done = bf16[2,16,2048]{2,1,0:T(8,128)(2,1)S(1)} collective-permute-done((bf16[2,16,2048]{2,1,0:T(8,128)(2,1)S(1)}, bf16[2,16,2048]{2,1,0:T(8,128)(2,1)S(1)}, u32[]{:S(2)}, u32[]{:S(2)}) %collective-permute-start) | collective-permute-done | bytes 131104 | tf_op jit(solution)/shard_map/while/body/eval_jaxpr/ppermute | solution.py:10
  44.8 1.6 %fusion.53 = f32[2,16,1,2]{3,2,1,0:T(1,128)S(1)} fusion(bf16[2,16,2,2048]{3,2,1,0:T(2,128)(2,1)} %get-tuple-element.510, bf16[2,16,2048,1]{2,1,0,3:T(8,128)(2,1)S(1)} %bitcast.83), kind=kOutput, calls=%fused_computation.6.clone.1 | convolution fusion | flops 262144 | bytes 393472 | tf_op jit(solution)/shard_map/while/body/eval_jaxpr/mtkd,mtd->mtk/dot_general | solution.py:27
  46.5 1.3 select_select_fusion.5
  47.8 1.3 collective-permute-start
  49.1 1.1 fusion.55
  50.3 3.8 %collective-permute-done = bf16[2,16,2048]{2,1,0:T(8,128)(2,1)S(1)} collective-permute-done((bf16[2,16,2048]{2,1,0:T(8,128)(2,1)S(1)}, bf16[2,16,2048]{2,1,0:T(8,128)(2,1)S(1)}, u32[]{:S(2)}, u32[]{:S(2)}) %collective-permute-start) | collective-permute-done | bytes 131104 | tf_op jit(solution)/shard_map/while/body/eval_jaxpr/ppermute | solution.py:10
  54.2 1.6 %fusion.53 = f32[2,16,1,2]{3,2,1,0:T(1,128)S(1)} fusion(bf16[2,16,2,2048]{3,2,1,0:T(2,128)(2,1)} %get-tuple-element.510, bf16[2,16,2048,1]{2,1,0,3:T(8,128)(2,1)S(1)} %bitcast.83), kind=kOutput, calls=%fused_computation.6.clone.1 | convolution fusion | flops 262144 | bytes 393472 | tf_op jit(solution)/shard_map/while/body/eval_jaxpr/mtkd,mtd->mtk/dot_general | solution.py:27
  55.9 1.3 select_select_fusion.5
  57.2 1.3 collective-permute-start
  58.5 1.1 fusion.55
  59.6 3.8 %collective-permute-done = bf16[2,16,2048]{2,1,0:T(8,128)(2,1)S(1)} collective-permute-done((bf16[2,16,2048]{2,1,0:T(8,128)(2,1)S(1)}, bf16[2,16,2048]{2,1,0:T(8,128)(2,1)S(1)}, u32[]{:S(2)}, u32[]{:S(2)}) %collective-permute-start) | collective-permute-done | bytes 131104 | tf_op jit(solution)/shard_map/while/body/eval_jaxpr/ppermute | solution.py:10
  63.5 1.6 %fusion.53 = f32[2,16,1,2]{3,2,1,0:T(1,128)S(1)} fusion(bf16[2,16,2,2048]{3,2,1,0:T(2,128)(2,1)} %get-tuple-element.510, bf16[2,16,2048,1]{2,1,0,3:T(8,128)(2,1)S(1)} %bitcast.83), kind=kOutput, calls=%fused_computation.6.clone.1 | convolution fusion | flops 262144 | bytes 393472 | tf_op jit(solution)/shard_map/while/body/eval_jaxpr/mtkd,mtd->mtk/dot_general | solution.py:27
  65.2 1.3 select_select_fusion.5
  66.5 1.3 collective-permute-start
  67.8 1.1 fusion.55
  69.0 3.8 %collective-permute-done = bf16[2,16,2048]{2,1,0:T(8,128)(2,1)S(1)} collective-permute-done((bf16[2,16,2048]{2,1,0:T(8,128)(2,1)S(1)}, bf16[2,16,2048]{2,1,0:T(8,128)(2,1)S(1)}, u32[]{:S(2)}, u32[]{:S(2)}) %collective-permute-start) | collective-permute-done | bytes 131104 | tf_op jit(solution)/shard_map/while/body/eval_jaxpr/ppermute | solution.py:10
  72.9 1.6 %fusion.53 = f32[2,16,1,2]{3,2,1,0:T(1,128)S(1)} fusion(bf16[2,16,2,2048]{3,2,1,0:T(2,128)(2,1)} %get-tuple-element.510, bf16[2,16,2048,1]{2,1,0,3:T(8,128)(2,1)S(1)} %bitcast.83), kind=kOutput, calls=%fused_computation.6.clone.1 | convolution fusion | flops 262144 | bytes 393472 | tf_op jit(solution)/shard_map/while/body/eval_jaxpr/mtkd,mtd->mtk/dot_general | solution.py:27
  74.6 1.3 select_select_fusion.5
  75.9 1.3 collective-permute-start
  77.2 1.1 fusion.55
  78.3 4.6 %collective-permute-done = bf16[2,16,2048]{2,1,0:T(8,128)(2,1)S(1)} collective-permute-done((bf16[2,16,2048]{2,1,0:T(8,128)(2,1)S(1)}, bf16[2,16,2048]{2,1,0:T(8,128)(2,1)S(1)}, u32[]{:S(2)}, u32[]{:S(2)}) %collective-permute-start) | collective-permute-done | bytes 131104 | tf_op jit(solution)/shard_map/while/body/eval_jaxpr/ppermute | solution.py:10
  84.2 14.3 %all_gather.3 = bf16[2,32,2048]{2,1,0:T(8,128)(2,1)S(1)} all-gather(bf16[2,8,2048]{2,1,0:T(8,128)(2,1)S(1)} %convolution_convert_fusion.1), channel_id=1, replica_groups=mesh['section'=8,'expert'=4] {'expert'}, dimensions={1}, use_global_device_ids=true | all-gather | bytes 327680 | tf_op jit(solution)/shard_map/all_gather | solution.py:92
  98.4 6.1 %fusion.16 = bf16[64,1792]{1,0:T(8,128)(2,1)} fusion(bf16[64,2048]{1,0:T(8,128)(2,1)S(1)} %bitcast.85, bf16[1,1792,2048]{2,1,0:T(8,128)(2,1)} %param.15), kind=kOutput, calls=%fused_computation.24 | convolution fusion | flops 469876736 | bytes 7831552 | tf_op jit(solution)/shard_map/dot_general | solution.py:94
  104.5 5.1 %fusion.15 = bf16[1,1792,2048]{1,2,0:T(8,128)(2,1)} fusion(bf16[64,2048]{1,0:T(8,128)(2,1)S(1)} %bitcast.86, bf16[64,1792]{1,0:T(8,128)(2,1)S(1)} %bitcast.82), kind=kOutput, calls=%fused_computation.23 | convolution fusion | flops 473432064 | bytes 7831552 | tf_op jit(solution)/shard_map/dot_general | solution.py:98
  109.6 10.4 %copy.14 = bf16[1,1792,2048]{2,1,0:T(8,128)(2,1)} copy(bf16[1,1792,2048]{1,2,0:T(8,128)(2,1)} %fusion.15) | data formatting | bytes 14680064
  120.1 7.9 %all-reduce.2.cloned.1.call-done = f32[2048,8]{0,1:T(8,128)} async-done(((f32[2048,8]{0,1:T(8,128)}), f32[2048,8]{0,1:T(8,128)}) %all-reduce.2.cloned.1.call-update) | async-done | bytes 65552 | tf_op jit(solution)/shard_map/psum | solution.py:84
  128.0 1.5 %multiply_bitcast_fusion = f32[1,2048,8]{1,2,0:T(8,128)} fusion(f32[2048,8]{0,1:T(8,128)} %all-reduce.2.cloned.1.call-done), kind=kLoop, calls=%fused_computation.31 | loop fusion | flops 16384 | bytes 131072 | tf_op jit(solution)/shard_map/broadcast_in_dim | solution.py:106
  (50 shorter events, 3.3 us)
Async XLA Ops:
  7.2 97.4 %copy-start = (bf16[1,2,32,1792]{3,2,1,0:T(8,128)(2,1)S(1)}, bf16[1,2,32,1792]{3,2,1,0:T(8,128)(2,1)}, u32[]{:S(2)}) copy-start(bf16[1,2,32,1792]{3,2,1,0:T(8,128)(2,1)} %param.14) | copy-start | bytes 688132
  7.2 120.8 %all-reduce.2.cloned.1.call-start = ((), (), s32[]{:S(2)}) async-start(), calls=%async_computation | async-start | bytes 131072 | tf_op jit(solution)/shard_map/psum | solution.py:84
  9.5 74.1 %copy-start.3 = (s32[1,2,16,2]{2,3,1,0:T(2,128)S(1)}, s32[1,2,16,2]{2,3,1,0:T(2,128)}, u32[]{:S(2)}) copy-start(s32[1,2,16,2]{2,3,1,0:T(2,128)} %param.13) | copy-start | bytes 772
  12.6 3.2 %collective-permute-start = (bf16[2,16,2048]{2,1,0:T(8,128)(2,1)S(1)}, bf16[2,16,2048]{2,1,0:T(8,128)(2,1)S(1)}, u32[]{:S(2)}, u32[]{:S(2)}) collective-permute-start(bf16[2,16,2048]{2,1,0:T(8,128)(2,1)S(1)} %get-tuple-element.469), channel_id=1, source_target_pairs={{4,0},{8,4},{12,8},{16,12},{20,16},{24,20},{28,24},{5,1},{9,5},{13... | collective-permute-start | bytes 393224 | tf_op jit(solution)/shard_map/while/body/eval_jaxpr/ppermute | solution.py:10
  18.9 7.2 %collective-permute-start = (bf16[2,16,2048]{2,1,0:T(8,128)(2,1)S(1)}, bf16[2,16,2048]{2,1,0:T(8,128)(2,1)S(1)}, u32[]{:S(2)}, u32[]{:S(2)}) collective-permute-start(bf16[2,16,2048]{2,1,0:T(8,128)(2,1)S(1)} %get-tuple-element.469), channel_id=1, source_target_pairs={{4,0},{8,4},{12,8},{16,12},{20,16},{24,20},{28,24},{5,1},{9,5},{13... | collective-permute-start | bytes 393224 | tf_op jit(solution)/shard_map/while/body/eval_jaxpr/ppermute | solution.py:10
  29.1 6.3 %collective-permute-start = (bf16[2,16,2048]{2,1,0:T(8,128)(2,1)S(1)}, bf16[2,16,2048]{2,1,0:T(8,128)(2,1)S(1)}, u32[]{:S(2)}, u32[]{:S(2)}) collective-permute-start(bf16[2,16,2048]{2,1,0:T(8,128)(2,1)S(1)} %get-tuple-element.469), channel_id=1, source_target_pairs={{4,0},{8,4},{12,8},{16,12},{20,16},{24,20},{28,24},{5,1},{9,5},{13... | collective-permute-start | bytes 393224 | tf_op jit(solution)/shard_map/while/body/eval_jaxpr/ppermute | solution.py:10
  38.5 6.3 %collective-permute-start = (bf16[2,16,2048]{2,1,0:T(8,128)(2,1)S(1)}, bf16[2,16,2048]{2,1,0:T(8,128)(2,1)S(1)}, u32[]{:S(2)}, u32[]{:S(2)}) collective-permute-start(bf16[2,16,2048]{2,1,0:T(8,128)(2,1)S(1)} %get-tuple-element.469), channel_id=1, source_target_pairs={{4,0},{8,4},{12,8},{16,12},{20,16},{24,20},{28,24},{5,1},{9,5},{13... | collective-permute-start | bytes 393224 | tf_op jit(solution)/shard_map/while/body/eval_jaxpr/ppermute | solution.py:10
  47.8 6.3 %collective-permute-start = (bf16[2,16,2048]{2,1,0:T(8,128)(2,1)S(1)}, bf16[2,16,2048]{2,1,0:T(8,128)(2,1)S(1)}, u32[]{:S(2)}, u32[]{:S(2)}) collective-permute-start(bf16[2,16,2048]{2,1,0:T(8,128)(2,1)S(1)} %get-tuple-element.469), channel_id=1, source_target_pairs={{4,0},{8,4},{12,8},{16,12},{20,16},{24,20},{28,24},{5,1},{9,5},{13... | collective-permute-start | bytes 393224 | tf_op jit(solution)/shard_map/while/body/eval_jaxpr/ppermute | solution.py:10
  57.2 6.3 %collective-permute-start = (bf16[2,16,2048]{2,1,0:T(8,128)(2,1)S(1)}, bf16[2,16,2048]{2,1,0:T(8,128)(2,1)S(1)}, u32[]{:S(2)}, u32[]{:S(2)}) collective-permute-start(bf16[2,16,2048]{2,1,0:T(8,128)(2,1)S(1)} %get-tuple-element.469), channel_id=1, source_target_pairs={{4,0},{8,4},{12,8},{16,12},{20,16},{24,20},{28,24},{5,1},{9,5},{13... | collective-permute-start | bytes 393224 | tf_op jit(solution)/shard_map/while/body/eval_jaxpr/ppermute | solution.py:10
  66.5 6.3 %collective-permute-start = (bf16[2,16,2048]{2,1,0:T(8,128)(2,1)S(1)}, bf16[2,16,2048]{2,1,0:T(8,128)(2,1)S(1)}, u32[]{:S(2)}, u32[]{:S(2)}) collective-permute-start(bf16[2,16,2048]{2,1,0:T(8,128)(2,1)S(1)} %get-tuple-element.469), channel_id=1, source_target_pairs={{4,0},{8,4},{12,8},{16,12},{20,16},{24,20},{28,24},{5,1},{9,5},{13... | collective-permute-start | bytes 393224 | tf_op jit(solution)/shard_map/while/body/eval_jaxpr/ppermute | solution.py:10
  75.9 7.1 %collective-permute-start = (bf16[2,16,2048]{2,1,0:T(8,128)(2,1)S(1)}, bf16[2,16,2048]{2,1,0:T(8,128)(2,1)S(1)}, u32[]{:S(2)}, u32[]{:S(2)}) collective-permute-start(bf16[2,16,2048]{2,1,0:T(8,128)(2,1)S(1)} %get-tuple-element.469), channel_id=1, source_target_pairs={{4,0},{8,4},{12,8},{16,12},{20,16},{24,20},{28,24},{5,1},{9,5},{13... | collective-permute-start | bytes 393224 | tf_op jit(solution)/shard_map/while/body/eval_jaxpr/ppermute | solution.py:10
  82.9 0.6 copy-start.2
  82.9 26.7 %copy-start.1 = (bf16[2,16,2048]{2,1,0:T(8,128)(2,1)}, bf16[2,16,2048]{2,1,0:T(8,128)(2,1)S(1)}, u32[]{:S(2)}) copy-start(bf16[2,16,2048]{2,1,0:T(8,128)(2,1)S(1)} %get-tuple-element.304) | copy-start | bytes 393220
Sparse Core Ops, SparseCore 0:
  83.7 44.2 all-reduce.1
where the time goes:
time: 138 us; the launch traced here: 136 us
  matrix products  45.1 us (33%)
  waiting for transfers between devices  37.2 us (27%)
  blocking collectives  14.3 us (10%)
  between operations  14.2 us (10%)
  local copies, waits for them, and re-layouts  12.5 us (9%)
  starting transfers between devices  10.4 us (8%)
  other arithmetic  2.4 us (2%)
    ppermute x8, waiting for transfers between devices, passed_along(): return lax.ppermute(value, axis, pairs)  29.3 us
    all_gather x1, blocking collectives, per_device(): gathered = lax.all_gather(rows_out, 'expert', axis=1, tiled=True)  14.3 us
    dot_general x8, matrix products, backprop(): jnp.einsum('mtkd,mtd->mtk', outputs, cotangent, preferred_element_type=jn...  12.8 us
    unnamed x9, local copies, waits for them, and re-layouts  11.1 us
    ppermute x8, starting transfers between devices, passed_along(): return lax.ppermute(value, axis, pairs)  10.3 us
    dot_general x8, matrix products, backprop(): jnp.einsum('mte,de->mtd', logit_grad, weights, precision=lax.Precision.HI...  10.3 us
    dot_general x8, matrix products, backprop(): jnp.einsum('mtd,mte->de', inputs.astype(jnp.float32), logit_grad, precisi...  9.18 us
    psum x1, waiting for transfers between devices, per_device(): router_grad = lax.psum(router_acc, 'expert') / total_tokens  7.93 us
  transfers between devices with their start and end apart: 9, of which 9 were waited for; matrix products, arithmetic and copies ran while one was open for 23% of the time, Pallas kernels for 0%

commit v1 on v0

--- a/solution.py
+++ b/solution.py
@@ -89,7 +89,8 @@
     weight = down_w[0]
     ff_local = weight.shape[0]
     slot_total = saved_hidden.shape[1]
-    gathered = lax.all_gather(rows_out, "expert", axis=1, tiled=True)
+    sent = jnp.stack([rows_out] * lax.axis_size("expert"))
+    gathered = jnp.concatenate(lax.all_to_all(sent, "expert", 0, 0), axis=1)
     flat_rows = gathered.reshape(-1, width)
     hidden_acc = lax.dot_general(
         flat_rows, weight, (((1,), (1,)), ((), ())), preferred_element_type=jnp.float32

time: 138 us -> 159 us (1.15)
  waiting for transfers between devices: 37.2 us -> 67.5 us
  blocking collectives: 14.3 us -> 0 us
  starting transfers between devices: 10.4 us -> 15.2 us
    psum x1, waiting for transfers between devices: 7.93 us -> 38.2 us  [per_device(): router_grad = lax.psum(router_acc, 'expert') / total_tokens]
    all_gather x1 -> x0, blocking collectives: 14.3 us -> none  [per_device(): gathered = lax.all_gather(rows_out, 'expert', axis=1, tiled=True)]
    all_to_all x0 -> x1, starting transfers between devices: none -> 4.87 us  [per_device(): gathered = jnp.concatenate(lax.all_to_all(sent, 'expert', 0, 0), axis=1)]
  transfers between devices with their start and end apart: 9 -> 10, of which waited for: 9 -> 9; matrix products, arithmetic and copies ran while one was open for 23% -> 8% of each run, Pallas kernels for 0% -> 0%
where the time goes in v1:
time: 159 us; the launch traced here: 158 us
  waiting for transfers between devices  67.5 us (42%)
  matrix products  45.1 us (28%)
  starting transfers between devices  15.2 us (10%)
  between operations  14.2 us (9%)
  local copies, waits for them, and re-layouts  13.2 us (8%)
  other arithmetic  2.4 us (2%)
    psum x1, waiting for transfers between devices, per_device(): router_grad = lax.psum(router_acc, 'expert') / total_tokens  38.2 us
    ppermute x8, waiting for transfers between devices, passed_along(): return lax.ppermute(value, axis, pairs)  29.3 us
    dot_general x8, matrix products, backprop(): jnp.einsum('mtkd,mtd->mtk', outputs, cotangent, preferred_element_type=jn...  12.8 us
    unnamed x9, local copies, waits for them, and re-layouts  11.1 us
    ppermute x8, starting transfers between devices, passed_along(): return lax.ppermute(value, axis, pairs)  10.3 us
    dot_general x8, matrix products, backprop(): jnp.einsum('mte,de->mtd', logit_grad, weights, precision=lax.Precision.HI...  10.3 us
    dot_general x8, matrix products, backprop(): jnp.einsum('mtd,mte->de', inputs.astype(jnp.float32), logit_grad, precisi...  9.18 us
    dot_general x1, matrix products, per_device(): lax.dot_general(flat_rows, weight, (((1,), (1,)), ((), ())), preferred_el...  6.12 us
  transfers between devices with their start and end apart: 10, of which 9 were waited for; matrix products, arithmetic and copies ran while one was open for 8% of the time, Pallas kernels for 0%

profile of v1, /device:TPU:0, one launch (start us, length us, event | category | flops | bytes accessed | tf_op | source)
XLA Modules:
  0.0 157.9 jit_solution(12226914277627411776)
XLA Ops:
  8.0 1.5 fusion.22
  9.5 73.4 %while.22 = (s32[]{:T(128)}, bf16[2,16,2048]{2,1,0:T(8,128)(2,1)S(1)}, bf16[2,16,2048]{2,1,0:T(8,128)(2,1)S(1)}, bf16[2,16,2048]{2,1,0:T(8,128)(2,1)S(1)}, f32[2...) while((s32[]{:T(128)}, ...), condition=%wide.region_2.3_spmd.clone, body=%wide.region_1.2_spmd.clone.sunk | while | flops 13419140 | bytes 2428622 | solution.py:80
  9.7 1.6 %fusion.53 = f32[2,16,1,2]{3,2,1,0:T(1,128)S(1)} fusion(bf16[2,16,2,2048]{3,2,1,0:T(2,128)(2,1)} %get-tuple-element.518, bf16[2,16,2048,1]{2,1,0,3:T(8,128)(2,1)S(1)} %bitcast.85), kind=kOutput, calls=%fused_computation.6.clone.1 | convolution fusion | flops 262144 | bytes 393472 | tf_op jit(solution)/shard_map/while/body/eval_jaxpr/mtkd,mtd->mtk/dot_general | solution.py:27
  11.3 1.3 select_select_fusion.5
  12.6 1.3 collective-permute-start
  13.9 1.1 fusion.55
  15.1 0.8 collective-permute-done
  15.9 1.6 %fusion.53 = f32[2,16,1,2]{3,2,1,0:T(1,128)S(1)} fusion(bf16[2,16,2,2048]{3,2,1,0:T(2,128)(2,1)} %get-tuple-element.518, bf16[2,16,2048,1]{2,1,0,3:T(8,128)(2,1)S(1)} %bitcast.85), kind=kOutput, calls=%fused_computation.6.clone.1 | convolution fusion | flops 262144 | bytes 393472 | tf_op jit(solution)/shard_map/while/body/eval_jaxpr/mtkd,mtd->mtk/dot_general | solution.py:27
  17.6 1.3 select_select_fusion.5
  18.9 1.3 collective-permute-start
  20.2 1.1 fusion.55
  21.4 4.7 %collective-permute-done = bf16[2,16,2048]{2,1,0:T(8,128)(2,1)S(1)} collective-permute-done((bf16[2,16,2048]{2,1,0:T(8,128)(2,1)S(1)}, bf16[2,16,2048]{2,1,0:T(8,128)(2,1)S(1)}, u32[]{:S(2)}, u32[]{:S(2)}) %collective-permute-start) | collective-permute-done | bytes 131104 | tf_op jit(solution)/shard_map/while/body/eval_jaxpr/ppermute | solution.py:10
  26.1 1.6 %fusion.53 = f32[2,16,1,2]{3,2,1,0:T(1,128)S(1)} fusion(bf16[2,16,2,2048]{3,2,1,0:T(2,128)(2,1)} %get-tuple-element.518, bf16[2,16,2048,1]{2,1,0,3:T(8,128)(2,1)S(1)} %bitcast.85), kind=kOutput, calls=%fused_computation.6.clone.1 | convolution fusion | flops 262144 | bytes 393472 | tf_op jit(solution)/shard_map/while/body/eval_jaxpr/mtkd,mtd->mtk/dot_general | solution.py:27
  27.8 1.3 select_select_fusion.5
  29.1 1.3 collective-permute-start
  30.4 1.1 fusion.55
  31.6 3.8 %collective-permute-done = bf16[2,16,2048]{2,1,0:T(8,128)(2,1)S(1)} collective-permute-done((bf16[2,16,2048]{2,1,0:T(8,128)(2,1)S(1)}, bf16[2,16,2048]{2,1,0:T(8,128)(2,1)S(1)}, u32[]{:S(2)}, u32[]{:S(2)}) %collective-permute-start) | collective-permute-done | bytes 131104 | tf_op jit(solution)/shard_map/while/body/eval_jaxpr/ppermute | solution.py:10
  35.5 1.6 %fusion.53 = f32[2,16,1,2]{3,2,1,0:T(1,128)S(1)} fusion(bf16[2,16,2,2048]{3,2,1,0:T(2,128)(2,1)} %get-tuple-element.518, bf16[2,16,2048,1]{2,1,0,3:T(8,128)(2,1)S(1)} %bitcast.85), kind=kOutput, calls=%fused_computation.6.clone.1 | convolution fusion | flops 262144 | bytes 393472 | tf_op jit(solution)/shard_map/while/body/eval_jaxpr/mtkd,mtd->mtk/dot_general | solution.py:27
  37.2 1.3 select_select_fusion.5
  38.5 1.3 collective-permute-start
  39.8 1.1 fusion.55
  40.9 3.8 %collective-permute-done = bf16[2,16,2048]{2,1,0:T(8,128)(2,1)S(1)} collective-permute-done((bf16[2,16,2048]{2,1,0:T(8,128)(2,1)S(1)}, bf16[2,16,2048]{2,1,0:T(8,128)(2,1)S(1)}, u32[]{:S(2)}, u32[]{:S(2)}) %collective-permute-start) | collective-permute-done | bytes 131104 | tf_op jit(solution)/shard_map/while/body/eval_jaxpr/ppermute | solution.py:10
  44.8 1.6 %fusion.53 = f32[2,16,1,2]{3,2,1,0:T(1,128)S(1)} fusion(bf16[2,16,2,2048]{3,2,1,0:T(2,128)(2,1)} %get-tuple-element.518, bf16[2,16,2048,1]{2,1,0,3:T(8,128)(2,1)S(1)} %bitcast.85), kind=kOutput, calls=%fused_computation.6.clone.1 | convolution fusion | flops 262144 | bytes 393472 | tf_op jit(solution)/shard_map/while/body/eval_jaxpr/mtkd,mtd->mtk/dot_general | solution.py:27
  46.5 1.3 select_select_fusion.5
  47.8 1.3 collective-permute-start
  49.1 1.1 fusion.55
  50.3 3.8 %collective-permute-done = bf16[2,16,2048]{2,1,0:T(8,128)(2,1)S(1)} collective-permute-done((bf16[2,16,2048]{2,1,0:T(8,128)(2,1)S(1)}, bf16[2,16,2048]{2,1,0:T(8,128)(2,1)S(1)}, u32[]{:S(2)}, u32[]{:S(2)}) %collective-permute-start) | collective-permute-done | bytes 131104 | tf_op jit(solution)/shard_map/while/body/eval_jaxpr/ppermute | solution.py:10
  54.2 1.6 %fusion.53 = f32[2,16,1,2]{3,2,1,0:T(1,128)S(1)} fusion(bf16[2,16,2,2048]{3,2,1,0:T(2,128)(2,1)} %get-tuple-element.518, bf16[2,16,2048,1]{2,1,0,3:T(8,128)(2,1)S(1)} %bitcast.85), kind=kOutput, calls=%fused_computation.6.clone.1 | convolution fusion | flops 262144 | bytes 393472 | tf_op jit(solution)/shard_map/while/body/eval_jaxpr/mtkd,mtd->mtk/dot_general | solution.py:27
  55.9 1.3 select_select_fusion.5
  57.2 1.3 collective-permute-start
  58.5 1.1 fusion.55
  59.6 3.8 %collective-permute-done = bf16[2,16,2048]{2,1,0:T(8,128)(2,1)S(1)} collective-permute-done((bf16[2,16,2048]{2,1,0:T(8,128)(2,1)S(1)}, bf16[2,16,2048]{2,1,0:T(8,128)(2,1)S(1)}, u32[]{:S(2)}, u32[]{:S(2)}) %collective-permute-start) | collective-permute-done | bytes 131104 | tf_op jit(solution)/shard_map/while/body/eval_jaxpr/ppermute | solution.py:10
  63.5 1.6 %fusion.53 = f32[2,16,1,2]{3,2,1,0:T(1,128)S(1)} fusion(bf16[2,16,2,2048]{3,2,1,0:T(2,128)(2,1)} %get-tuple-element.518, bf16[2,16,2048,1]{2,1,0,3:T(8,128)(2,1)S(1)} %bitcast.85), kind=kOutput, calls=%fused_computation.6.clone.1 | convolution fusion | flops 262144 | bytes 393472 | tf_op jit(solution)/shard_map/while/body/eval_jaxpr/mtkd,mtd->mtk/dot_general | solution.py:27
  65.2 1.3 select_select_fusion.5
  66.5 1.3 collective-permute-start
  67.8 1.1 fusion.55
  69.0 3.8 %collective-permute-done = bf16[2,16,2048]{2,1,0:T(8,128)(2,1)S(1)} collective-permute-done((bf16[2,16,2048]{2,1,0:T(8,128)(2,1)S(1)}, bf16[2,16,2048]{2,1,0:T(8,128)(2,1)S(1)}, u32[]{:S(2)}, u32[]{:S(2)}) %collective-permute-start) | collective-permute-done | bytes 131104 | tf_op jit(solution)/shard_map/while/body/eval_jaxpr/ppermute | solution.py:10
  72.9 1.6 %fusion.53 = f32[2,16,1,2]{3,2,1,0:T(1,128)S(1)} fusion(bf16[2,16,2,2048]{3,2,1,0:T(2,128)(2,1)} %get-tuple-element.518, bf16[2,16,2048,1]{2,1,0,3:T(8,128)(2,1)S(1)} %bitcast.85), kind=kOutput, calls=%fused_computation.6.clone.1 | convolution fusion | flops 262144 | bytes 393472 | tf_op jit(solution)/shard_map/while/body/eval_jaxpr/mtkd,mtd->mtk/dot_general | solution.py:27
  74.6 1.3 select_select_fusion.5
  75.9 1.3 collective-permute-start
  77.2 1.1 fusion.55
  78.3 4.6 %collective-permute-done = bf16[2,16,2048]{2,1,0:T(8,128)(2,1)S(1)} collective-permute-done((bf16[2,16,2048]{2,1,0:T(8,128)(2,1)S(1)}, bf16[2,16,2048]{2,1,0:T(8,128)(2,1)S(1)}, u32[]{:S(2)}, u32[]{:S(2)}) %collective-permute-start) | collective-permute-done | bytes 131104 | tf_op jit(solution)/shard_map/while/body/eval_jaxpr/ppermute | solution.py:10
  84.9 4.9 %all-to-all-start = ((bf16[4,2,8,2048]{3,2,1,0:T(8,128)(2,1)}), bf16[4,2,8,2048]{3,2,1,0:T(8,128)(2,1)S(1)}, u32[]{:S(2)}, u32[]{:S(2)}) async-start(bf16[4,2,8,2048]{3,2,1,0:T(8,128)(2,1)} %stack.3), calls=%async_computation | async-start | bytes 524288 | tf_op jit(solution)/shard_map/all_to_all | solution.py:93
  89.7 38.2 %all-reduce.2.cloned.1.call-done = f32[2048,8]{0,1:T(8,128)} async-done(((f32[2048,8]{0,1:T(8,128)}), f32[2048,8]{0,1:T(8,128)}) %all-reduce.2.cloned.1.call-update) | async-done | bytes 65552 | tf_op jit(solution)/shard_map/psum | solution.py:84
  127.9 1.5 multiply_bitcast_fusion
  129.4 6.1 %fusion.16 = bf16[64,1792]{1,0:T(8,128)(2,1)} fusion(bf16[64,2048]{1,0:T(8,128)(2,1)S(1)} %bitcast.87, bf16[1,1792,2048]{2,1,0:T(8,128)(2,1)} %param.15), kind=kOutput, calls=%fused_computation.24 | convolution fusion | flops 469876736 | bytes 7831552 | tf_op jit(solution)/shard_map/dot_general | solution.py:95
  135.5 5.1 %fusion.15 = bf16[1,1792,2048]{1,2,0:T(8,128)(2,1)} fusion(bf16[64,2048]{1,0:T(8,128)(2,1)S(1)} %bitcast.88, bf16[64,1792]{1,0:T(8,128)(2,1)S(1)} %bitcast.84), kind=kOutput, calls=%fused_computation.23 | convolution fusion | flops 473432064 | bytes 7831552 | tf_op jit(solution)/shard_map/dot_general | solution.py:99
  140.6 10.4 %copy.23 = bf16[1,1792,2048]{2,1,0:T(8,128)(2,1)} copy(bf16[1,1792,2048]{1,2,0:T(8,128)(2,1)} %fusion.15) | data formatting | bytes 14680064
  (53 shorter events, 4.1 us)
Async XLA Ops:
  7.2 128.4 %copy-start = (bf16[1,2,32,1792]{3,2,1,0:T(8,128)(2,1)S(1)}, bf16[1,2,32,1792]{3,2,1,0:T(8,128)(2,1)}, u32[]{:S(2)}) copy-start(bf16[1,2,32,1792]{3,2,1,0:T(8,128)(2,1)} %param.14) | copy-start | bytes 688132
  7.2 120.7 %all-reduce.2.cloned.1.call-start = ((), (), s32[]{:S(2)}) async-start(), calls=%async_computation.1 | async-start | bytes 131072 | tf_op jit(solution)/shard_map/psum | solution.py:84
  9.5 74.1 %copy-start.3 = (s32[1,2,16,2]{2,3,1,0:T(2,128)S(1)}, s32[1,2,16,2]{2,3,1,0:T(2,128)}, u32[]{:S(2)}) copy-start(s32[1,2,16,2]{2,3,1,0:T(2,128)} %param.13) | copy-start | bytes 772
  12.6 3.2 %collective-permute-start = (bf16[2,16,2048]{2,1,0:T(8,128)(2,1)S(1)}, bf16[2,16,2048]{2,1,0:T(8,128)(2,1)S(1)}, u32[]{:S(2)}, u32[]{:S(2)}) collective-permute-start(bf16[2,16,2048]{2,1,0:T(8,128)(2,1)S(1)} %get-tuple-element.477), channel_id=1, source_target_pairs={{4,0},{8,4},{12,8},{16,12},{20,16},{24,20},{28,24},{5,1},{9,5},{13... | collective-permute-start | bytes 393224 | tf_op jit(solution)/shard_map/while/body/eval_jaxpr/ppermute | solution.py:10
  18.9 7.2 %collective-permute-start = (bf16[2,16,2048]{2,1,0:T(8,128)(2,1)S(1)}, bf16[2,16,2048]{2,1,0:T(8,128)(2,1)S(1)}, u32[]{:S(2)}, u32[]{:S(2)}) collective-permute-start(bf16[2,16,2048]{2,1,0:T(8,128)(2,1)S(1)} %get-tuple-element.477), channel_id=1, source_target_pairs={{4,0},{8,4},{12,8},{16,12},{20,16},{24,20},{28,24},{5,1},{9,5},{13... | collective-permute-start | bytes 393224 | tf_op jit(solution)/shard_map/while/body/eval_jaxpr/ppermute | solution.py:10
  29.1 6.3 %collective-permute-start = (bf16[2,16,2048]{2,1,0:T(8,128)(2,1)S(1)}, bf16[2,16,2048]{2,1,0:T(8,128)(2,1)S(1)}, u32[]{:S(2)}, u32[]{:S(2)}) collective-permute-start(bf16[2,16,2048]{2,1,0:T(8,128)(2,1)S(1)} %get-tuple-element.477), channel_id=1, source_target_pairs={{4,0},{8,4},{12,8},{16,12},{20,16},{24,20},{28,24},{5,1},{9,5},{13... | collective-permute-start | bytes 393224 | tf_op jit(solution)/shard_map/while/body/eval_jaxpr/ppermute | solution.py:10
  38.5 6.3 %collective-permute-start = (bf16[2,16,2048]{2,1,0:T(8,128)(2,1)S(1)}, bf16[2,16,2048]{2,1,0:T(8,128)(2,1)S(1)}, u32[]{:S(2)}, u32[]{:S(2)}) collective-permute-start(bf16[2,16,2048]{2,1,0:T(8,128)(2,1)S(1)} %get-tuple-element.477), channel_id=1, source_target_pairs={{4,0},{8,4},{12,8},{16,12},{20,16},{24,20},{28,24},{5,1},{9,5},{13... | collective-permute-start | bytes 393224 | tf_op jit(solution)/shard_map/while/body/eval_jaxpr/ppermute | solution.py:10
  47.8 6.3 %collective-permute-start = (bf16[2,16,2048]{2,1,0:T(8,128)(2,1)S(1)}, bf16[2,16,2048]{2,1,0:T(8,128)(2,1)S(1)}, u32[]{:S(2)}, u32[]{:S(2)}) collective-permute-start(bf16[2,16,2048]{2,1,0:T(8,128)(2,1)S(1)} %get-tuple-element.477), channel_id=1, source_target_pairs={{4,0},{8,4},{12,8},{16,12},{20,16},{24,20},{28,24},{5,1},{9,5},{13... | collective-permute-start | bytes 393224 | tf_op jit(solution)/shard_map/while/body/eval_jaxpr/ppermute | solution.py:10
  57.2 6.3 %collective-permute-start = (bf16[2,16,2048]{2,1,0:T(8,128)(2,1)S(1)}, bf16[2,16,2048]{2,1,0:T(8,128)(2,1)S(1)}, u32[]{:S(2)}, u32[]{:S(2)}) collective-permute-start(bf16[2,16,2048]{2,1,0:T(8,128)(2,1)S(1)} %get-tuple-element.477), channel_id=1, source_target_pairs={{4,0},{8,4},{12,8},{16,12},{20,16},{24,20},{28,24},{5,1},{9,5},{13... | collective-permute-start | bytes 393224 | tf_op jit(solution)/shard_map/while/body/eval_jaxpr/ppermute | solution.py:10
  66.5 6.3 %collective-permute-start = (bf16[2,16,2048]{2,1,0:T(8,128)(2,1)S(1)}, bf16[2,16,2048]{2,1,0:T(8,128)(2,1)S(1)}, u32[]{:S(2)}, u32[]{:S(2)}) collective-permute-start(bf16[2,16,2048]{2,1,0:T(8,128)(2,1)S(1)} %get-tuple-element.477), channel_id=1, source_target_pairs={{4,0},{8,4},{12,8},{16,12},{20,16},{24,20},{28,24},{5,1},{9,5},{13... | collective-permute-start | bytes 393224 | tf_op jit(solution)/shard_map/while/body/eval_jaxpr/ppermute | solution.py:10
  75.9 7.1 %collective-permute-start = (bf16[2,16,2048]{2,1,0:T(8,128)(2,1)S(1)}, bf16[2,16,2048]{2,1,0:T(8,128)(2,1)S(1)}, u32[]{:S(2)}, u32[]{:S(2)}) collective-permute-start(bf16[2,16,2048]{2,1,0:T(8,128)(2,1)S(1)} %get-tuple-element.477), channel_id=1, source_target_pairs={{4,0},{8,4},{12,8},{16,12},{20,16},{24,20},{28,24},{5,1},{9,5},{13... | collective-permute-start | bytes 393224 | tf_op jit(solution)/shard_map/while/body/eval_jaxpr/ppermute | solution.py:10
  82.9 0.6 copy-start.2
  82.9 57.6 %copy-start.1 = (bf16[2,16,2048]{2,1,0:T(8,128)(2,1)}, bf16[2,16,2048]{2,1,0:T(8,128)(2,1)S(1)}, u32[]{:S(2)}) copy-start(bf16[2,16,2048]{2,1,0:T(8,128)(2,1)S(1)} %get-tuple-element.304) | copy-start | bytes 393220
  84.9 44.5 %all-to-all-start = ((bf16[4,2,8,2048]{3,2,1,0:T(8,128)(2,1)}), bf16[4,2,8,2048]{3,2,1,0:T(8,128)(2,1)S(1)}, u32[]{:S(2)}, u32[]{:S(2)}) async-start(bf16[4,2,8,2048]{3,2,1,0:T(8,128)(2,1)} %stack.3), calls=%async_computation | async-start | bytes 524288 | tf_op jit(solution)/shard_map/all_to_all | solution.py:93
Sparse Core Ops, SparseCore 0:
  83.7 44.1 all-reduce.1
